TPU v7x, 32 devices: a whole 2x2x4 slice. The times are simulated.
32 devices in a mesh: gx: 4 (over y, x), gy: 4 (over z), row: 2 (over core).
Axes of the slice: x: 2, y: 2, z: 4, core: 2. Of those that a mesh axis runs over, the one named last changes fastest.
Arguments:
- columns: bfloat16 [137, 131072], P(None, ('gx', 'gy')), may hold values from -6 to 6
- level_weights: bfloat16 [137, 16], replicated, may hold values from -0.5 to 0.5
- orbit_term: float32 [16, 32], replicated, may hold values from -6 to 6
- col_owner: int32 [524288, 1], P(('gx', 'gy', 'row')), may hold values from 0 to 15; in each aligned block of 16384 rows (0 to 16383, 16384 to 32767, ...) at most 2048 rows name the same one
- col_local: int32 [524288], P(('gx', 'gy', 'row')), may hold values from 0 to 8191
- orbit_bin: int32 [524288], P(('gx', 'gy', 'row')), may hold values from 0 to 31
- group_id: int32 [524288], P(('gx', 'gy', 'row')), may hold values from 0 to 63
- departure: float32 [524288], P(('gx', 'gy', 'row')), may hold values from -6 to 6
Outputs:
- covariance: float32 [16, 16, 64], P(None, None, 'row')
- cross: float32 [16, 64], P(None, 'row')
Inputs may be any that keep to these rules, and one draw needn't show every extreme that they name: `col_owner`: among the footprints of one device, no owning device is named more than 2048 times; some owning device is named exactly 2048 times.
All inputs are finite; a program needn't handle non-finite values.
Results may differ from a plain program's by a relative error of at most 0.0022.
Values may be sent and summed in bfloat16 or wider, within the bound.
A program may use at most 128 MiB of HBM per device.

v0:
```python
import math
import jax
import jax.numpy as jnp
from jax import lax
from jax.sharding import PartitionSpec as P

NGRP = 64


def send_request(wanted):
    return lax.all_to_all(wanted, ("gx", "gy"), split_axis=0, concat_axis=0, tiled=True)


def send_answer(picked):
    return lax.all_to_all(picked, ("gx", "gy"), split_axis=1, concat_axis=1, tiled=True)


def local(columns, level_weights, orbit_term, col_owner, col_local, orbit_bin, group_id, departure):
    grid_x = lax.axis_size("gx")
    grid_y = lax.axis_size("gy")
    owners = grid_x * grid_y
    footprints = col_owner.shape[0]
    capacity = 2 * footprints // owners
    slots_all = owners * capacity
    npred = level_weights.shape[1]
    ngroups = NGRP
    owner = col_owner[:, 0]
    owner_hits = (owner[:, None] == jnp.arange(owners, dtype=jnp.int32)[None, :]).astype(jnp.int32)
    ranks = jnp.cumsum(owner_hits, axis=0)
    slot = jnp.sum(ranks * owner_hits, axis=1) - 1
    target = owner * capacity + slot
    stacked = jnp.stack([col_local, orbit_bin, group_id], axis=0)
    placed = jnp.full((3, slots_all), -1, jnp.int32).at[:, target].set(stacked)
    slot_depart = jnp.zeros((slots_all,), jnp.float32).at[target].set(departure)
    wanted = jnp.maximum(placed[0], 0).reshape(owners, capacity)
    asked = send_request(wanted)
    thickness = jnp.dot(level_weights.T, columns, preferred_element_type=jnp.float32).astype(
        jnp.bfloat16
    )
    picked = thickness[:, asked]
    back = send_answer(picked)
    flat = back.reshape(npred, slots_all)
    slot_bin = placed[1]
    slot_group = placed[2]
    width = math.gcd(slots_all, 4096)
    nblocks = slots_all // width
    bin_range = jnp.arange(orbit_term.shape[1], dtype=jnp.int32)
    group_range = jnp.arange(ngroups, dtype=jnp.int32)

    def accumulate(carry, which):
        prod_acc, sum_acc, count_acc = carry
        first = which * width
        part_flat = lax.dynamic_slice_in_dim(flat, first, width, 1)
        part_bin = lax.dynamic_slice_in_dim(slot_bin, first, width, 0)
        grp = lax.dynamic_slice_in_dim(slot_group, first, width, 0)
        dep = lax.dynamic_slice_in_dim(slot_depart, first, width, 0)
        bin_hits = (bin_range[:, None] == part_bin[None, :]).astype(jnp.float32)
        block = part_flat.astype(jnp.float32) + jnp.dot(
            orbit_term,
            bin_hits,
            precision=lax.Precision.HIGHEST,
            preferred_element_type=jnp.float32,
        )
        hits = (grp[:, None] == group_range[None, :]).astype(jnp.float32)
        outer = (block[:, None, :] * block[None, :, :]).reshape(npred * npred, width)
        prod_acc = prod_acc + jnp.dot(
            outer, hits, precision=lax.Precision.HIGHEST, preferred_element_type=jnp.float32
        )
        sum_acc = sum_acc + jnp.dot(
            block * dep[None, :],
            hits,
            precision=lax.Precision.HIGHEST,
            preferred_element_type=jnp.float32,
        )
        count_acc = count_acc + jnp.sum(hits, axis=0)[None, :]
        return ((prod_acc, sum_acc, count_acc), None)

    start = (
        jnp.zeros((npred * npred, ngroups), jnp.float32),
        jnp.zeros((npred, ngroups), jnp.float32),
        jnp.zeros((1, ngroups), jnp.float32),
    )
    (products, sums, count), _ = lax.scan(accumulate, start, jnp.arange(nblocks, dtype=jnp.int32))
    share = ngroups // lax.axis_size("row")
    products, sums, count = (
        lax.psum_scatter(products, "row", scatter_dimension=1, tiled=True),
        lax.psum_scatter(sums, "row", scatter_dimension=1, tiled=True),
        lax.psum_scatter(count, "row", scatter_dimension=1, tiled=True),
    )
    products, sums, count = lax.psum((products, sums, count), ("gx", "gy"))
    scale = 1.0 / (count + 1.0)
    covariance = (products * scale).reshape(npred, npred, share)
    cross = sums * scale
    return (covariance, cross)


def solution(mesh):
    in_specs = (
        P(None, ("gx", "gy")),
        P(),
        P(),
        P(("gx", "gy", "row"), None),
        P(("gx", "gy", "row")),
        P(("gx", "gy", "row")),
        P(("gx", "gy", "row")),
        P(("gx", "gy", "row")),
    )
    out_specs = (P(None, None, "row"), P(None, "row"))
    return jax.shard_map(local, mesh=mesh, in_specs=in_specs, out_specs=out_specs, check_vma=False)
```

profile of v0, /device:TPU:0, one launch (start us, length us, event | category | flops | bytes accessed | tf_op | source)
XLA Modules:
  0.0 520.1 jit_solution(6604722221456737863)
XLA Ops:
  7.2 1.1 copy.35
  8.7 1.1 broadcast_add_fusion
  9.8 1.6 copy.36
  11.4 1.6 fusion.17
  13.0 0.9 compare_select_fusion.1
  14.0 1.1 add_bitcast_fusion
  15.1 5.1 copy.37
  20.1 47.4 %scatter_custom_fusion = s32[3,32768]{0,1:T(8,128)} fusion(s32[16384]{0:T(1024)S(1)} %bitcast.78, s32[16384,3]{1,0:T(8,128)} %copy.37, s32[]{:T(128)} %constant.6.clone.1), kind=kCustom, calls=%fused_computation.26 | custom fusion | bytes 393728 | tf_op jit(solution)/shard_map/scatter | solution.py:33
  67.5 30.9 %slice_reduce_fusion = (s32[32768]{0:T(1024)}, s32[32768]{0:T(1024)}, s32[32768]{0:T(1024)}) fusion(s32[3,32768]{0,1:T(8,128)} %scatter_custom_fusion), kind=kLoop, calls=%fused_computation.21 | loop fusion | flops 32768 | bytes 786432 | tf_op jit(solution)/shard_map/slice | solution.py:44
  98.4 8.3 %all-to-all-start = ((s32[16,1,2048]{2,1,0:T(1,128)}), s32[16,1,2048]{2,1,0:T(1,128)S(1)}, u32[]{:S(2)}, u32[]{:S(2)}) async-start(s32[16,1,2048]{2,1,0:T(1,128)} %bitcast.24), calls=%async_computation | async-start | bytes 262144 | tf_op jit(solution)/shard_map/all_to_all | solution.py:11
  107.2 1.8 copy.39
  109.0 5.5 %all-to-all-done = s32[16,1,2048]{2,1,0:T(1,128)S(1)} async-done(((s32[16,1,2048]{2,1,0:T(1,128)}), s32[16,1,2048]{2,1,0:T(1,128)S(1)}, u32[]{:S(2)}, u32[]{:S(2)}) %all-to-all-start) | async-done | bytes 131104 | tf_op jit(solution)/shard_map/all_to_all | solution.py:11
  114.6 111.2 %gather_fusion = bf16[32768,16]{1,0:T(8,128)(2,1)} fusion(bf16[16,8192]{0,1:T(8,128)(2,1)} %copy.39, s32[32768]{0:T(1024)S(1)} %broadcast_clamp_fusion), kind=kCustom, calls=%fused_computation | custom fusion | bytes 2228224 | tf_op jit(solution)/shard_map/gather | solution.py:40
  225.8 7.8 %copy.40 = bf16[16,2048,16]{1,2,0:T(8,128)(2,1)} copy(bf16[16,2048,16]{2,1,0:T(8,128)(2,1)} %bitcast.64) | data formatting | bytes 2097152 | tf_op jit(solution)/shard_map/gather | solution.py:40
  233.6 3.7 all-to-all-start.1
  237.4 61.1 %scatter_custom_fusion.1 = f32[32768]{0:T(1024)} fusion(s32[16384]{0:T(1024)S(1)} %bitcast.79, f32[16384]{0:T(1024)} %param.17, f32[]{:T(128)} %constant.20.clone.1), kind=kCustom, calls=%fused_computation.41 | custom fusion | bytes 131584 | tf_op jit(solution)/shard_map/scatter | solution.py:34
  298.5 1.0 copy.47
  299.6 103.2 %while.15 = (s32[]{:T(128)}, f32[256,64]{0,1:T(8,128)S(1)}, f32[16,64]{1,0:T(8,128)}, f32[1,64]{1,0:T(1,128)S(1)}, s32[8]{0:T(128)S(1)}, /*index=5*/bf16[16,3276...) while((s32[]{:T(128)}, f32[256,64]{0,1:T(8,128)S(1)}, ...), condition=%wide.region_7.8_spmd.clone, body=%wide.region_5.7_spmd.clone.sunk | while | flops 883525696 | bytes 9661715 | solution.py:83
  300.9 0.7 dynamic_slice.29
  301.6 1.2 fusion.36
  302.8 2.4 broadcast_multiply_fusion.4
  306.0 4.5 convolution_add_fusion.4
  310.5 0.7 dynamic_slice.31
  313.8 0.7 dynamic_slice.29
  314.5 1.2 fusion.36
  315.7 2.4 broadcast_multiply_fusion.4
  318.9 4.5 convolution_add_fusion.4
  323.4 0.7 dynamic_slice.31
  326.7 0.7 dynamic_slice.29
  327.4 1.2 fusion.36
  328.6 2.4 broadcast_multiply_fusion.4
  331.8 4.5 convolution_add_fusion.4
  336.3 0.7 dynamic_slice.31
  339.6 0.7 dynamic_slice.29
  340.3 1.2 fusion.36
  341.5 2.4 broadcast_multiply_fusion.4
  344.7 4.5 convolution_add_fusion.4
  349.2 0.7 dynamic_slice.31
  352.5 0.7 dynamic_slice.29
  353.2 1.2 fusion.36
  354.4 2.4 broadcast_multiply_fusion.4
  357.6 4.5 convolution_add_fusion.4
  362.1 0.7 dynamic_slice.31
  365.4 0.7 dynamic_slice.29
  366.1 1.2 fusion.36
  367.3 2.4 broadcast_multiply_fusion.4
  370.5 4.5 convolution_add_fusion.4
  375.0 0.7 dynamic_slice.31
  378.3 0.7 dynamic_slice.29
  379.0 1.2 fusion.36
  380.2 2.4 broadcast_multiply_fusion.4
  383.4 4.5 convolution_add_fusion.4
  387.9 0.7 dynamic_slice.31
  391.9 1.2 fusion.36
  393.1 2.4 broadcast_multiply_fusion.4
  396.3 4.5 convolution_add_fusion.4
  403.5 1.4 copy.45
  405.7 6.7 %reduce-scatter.10.cloned.1.call-done = f32[32,1]{1,0:T(8,128)} async-done(((f32[64,1]{1,0:T(8,128)}), f32[32,1]{1,0:T(8,128)}) %reduce-scatter.10.cloned.1.call-update) | async-done | bytes 144
  412.4 0.8 copy.44
  413.2 10.1 %reduce-scatter.12.cloned.1.call-done = f32[32,16]{1,0:T(8,128)} async-done(((f32[64,16]{1,0:T(8,128)}), f32[32,16]{1,0:T(8,128)}) %reduce-scatter.12.cloned.1.call-update) | async-done | bytes 2064
  423.3 0.8 copy.46
  424.1 10.7 %reduce-scatter.8.cloned.1.call-done = f32[256,32]{0,1:T(8,128)} async-done(((f32[256,64]{0,1:T(8,128)}), f32[256,32]{0,1:T(8,128)}) %reduce-scatter.8.cloned.1.call-update) | async-done | bytes 32784 | tf_op jit(solution)/shard_map/reduce_scatter | solution.py:86
  434.7 77.4 %all-reduce = (f32[256,32]{0,1:T(8,128)S(1)}, f32[1,32]{1,0:T(1,128)S(1)}, f32[16,32]{1,0:T(8,128)S(1)}) all-reduce(f32[256,32]{0,1:T(8,128)} %reduce-scatter.8.cloned.1.call-done, f32[1,32]{1,0:T(1,128)S(1)} %copy.44, f32[16,32]{1,0:T(8,128)S(1)} %copy.46), channel_id=1, replica_groups=mesh['gx'=4,'gy'=4,'row'=2] {'gx','gy'}, use_global_device_ids=true, to_apply=%region_9.10 | all-reduce | flops 8736 | bytes 69888 | tf_op jit(solution)/shard_map/psum | solution.py:90
  512.8 0.8 copy.42
  (105 shorter events, 25.6 us)
Async XLA Ops:
  7.2 99.6 %copy-start = (bf16[137,8192]{1,0:T(8,128)(2,1)S(1)}, bf16[137,8192]{1,0:T(8,128)(2,1)}, u32[]{:S(2)}) copy-start(bf16[137,8192]{1,0:T(8,128)(2,1)} %param.10) | copy-start | bytes 6733828
  67.5 39.3 %copy-start.3 = (bf16[137,16]{0,1:T(8,128)(2,1)S(1)}, bf16[137,16]{0,1:T(8,128)(2,1)}, u32[]{:S(2)}) copy-start(bf16[137,16]{0,1:T(8,128)(2,1)} %param.11) | copy-start | bytes 13156
  98.4 16.0 %all-to-all-start = ((s32[16,1,2048]{2,1,0:T(1,128)}), s32[16,1,2048]{2,1,0:T(1,128)S(1)}, u32[]{:S(2)}, u32[]{:S(2)}) async-start(s32[16,1,2048]{2,1,0:T(1,128)} %bitcast.24), calls=%async_computation | async-start | bytes 262144 | tf_op jit(solution)/shard_map/all_to_all | solution.py:11
  225.8 73.7 %copy-start.2 = (f32[16,32]{1,0:T(8,128)S(1)}, f32[16,32]{1,0:T(8,128)}, u32[]{:S(2)}) copy-start(f32[16,32]{1,0:T(8,128)} %param.12) | copy-start | bytes 6148
  233.6 64.9 %all-to-all-start.1 = ((bf16[16,16,2048]{2,0,1:T(8,128)(2,1)}), bf16[16,16,2048]{2,0,1:T(8,128)(2,1)S(1)}, u32[]{:S(2)}, u32[]{:S(2)}) async-start(bf16[16,16,2048]{2,0,1:T(8,128)(2,1)} %bitcast.13), calls=%async_computation.1 | async-start | bytes 2097152 | tf_op jit(solution)/shard_map/all_to_all | solution.py:15
  237.3 175.1 %reduce-scatter.10.cloned.1.call-start = ((), (), s32[]{:S(2)}) async-start(), calls=%async_computation.6 | async-start | bytes 49152
  299.6 11.7 %copy-start.4 = (f32[16,64]{1,0:T(8,128)S(1)}, f32[16,64]{1,0:T(8,128)}, u32[]{:S(2)}) copy-start(f32[16,64]{1,0:T(8,128)} %get-tuple-element.209) | copy-start | bytes 12292 | tf_op jit(solution)/shard_map/while
  311.8 0.6 copy-start.5
  312.5 11.7 %copy-start.4 = (f32[16,64]{1,0:T(8,128)S(1)}, f32[16,64]{1,0:T(8,128)}, u32[]{:S(2)}) copy-start(f32[16,64]{1,0:T(8,128)} %get-tuple-element.209) | copy-start | bytes 12292 | tf_op jit(solution)/shard_map/while
  324.7 0.6 copy-start.5
  325.4 11.7 %copy-start.4 = (f32[16,64]{1,0:T(8,128)S(1)}, f32[16,64]{1,0:T(8,128)}, u32[]{:S(2)}) copy-start(f32[16,64]{1,0:T(8,128)} %get-tuple-element.209) | copy-start | bytes 12292 | tf_op jit(solution)/shard_map/while
  337.6 0.6 copy-start.5
  338.2 11.7 %copy-start.4 = (f32[16,64]{1,0:T(8,128)S(1)}, f32[16,64]{1,0:T(8,128)}, u32[]{:S(2)}) copy-start(f32[16,64]{1,0:T(8,128)} %get-tuple-element.209) | copy-start | bytes 12292 | tf_op jit(solution)/shard_map/while
  350.5 0.6 copy-start.5
  351.1 11.7 %copy-start.4 = (f32[16,64]{1,0:T(8,128)S(1)}, f32[16,64]{1,0:T(8,128)}, u32[]{:S(2)}) copy-start(f32[16,64]{1,0:T(8,128)} %get-tuple-element.209) | copy-start | bytes 12292 | tf_op jit(solution)/shard_map/while
  363.4 0.6 copy-start.5
  364.1 11.7 %copy-start.4 = (f32[16,64]{1,0:T(8,128)S(1)}, f32[16,64]{1,0:T(8,128)}, u32[]{:S(2)}) copy-start(f32[16,64]{1,0:T(8,128)} %get-tuple-element.209) | copy-start | bytes 12292 | tf_op jit(solution)/shard_map/while
  376.3 0.6 copy-start.5
  376.9 11.7 %copy-start.4 = (f32[16,64]{1,0:T(8,128)S(1)}, f32[16,64]{1,0:T(8,128)}, u32[]{:S(2)}) copy-start(f32[16,64]{1,0:T(8,128)} %get-tuple-element.209) | copy-start | bytes 12292 | tf_op jit(solution)/shard_map/while
  389.2 0.6 copy-start.5
  389.8 11.7 %copy-start.4 = (f32[16,64]{1,0:T(8,128)S(1)}, f32[16,64]{1,0:T(8,128)}, u32[]{:S(2)}) copy-start(f32[16,64]{1,0:T(8,128)} %get-tuple-element.209) | copy-start | bytes 12292 | tf_op jit(solution)/shard_map/while
  402.1 0.6 copy-start.5
  402.7 2.2 copy-start.1
  403.5 19.8 %reduce-scatter.12.cloned.1.call-start = ((), (), s32[]{:S(2)}) async-start(), calls=%async_computation.7 | async-start | bytes 49152
  404.9 29.8 %reduce-scatter.8.cloned.1.call-start = ((), (), s32[]{:S(2)}) async-start(), calls=%async_computation.5 | async-start | bytes 98304 | tf_op jit(solution)/shard_map/reduce_scatter | solution.py:86
Sparse Core Ops, SparseCore 0:
  403.6 8.7 reduce-scatter.9
  414.6 8.6 reduce-scatter.11
  426.0 8.6 reduce-scatter.7
where the time goes:
time: 523 us; the launch traced here: 520 us
  local copies, waits for them, and re-layouts  268 us (51%)
  blocking collectives  77.4 us (15%)
  other arithmetic  57.9 us (11%)
  matrix products  51.1 us (10%)
  waiting for transfers between devices  33.7 us (6%)
  between operations  13.9 us (3%)
  starting transfers between devices  12.1 us (2%)
  loops' own time  5.87 us (1%)
    gather x2, local copies, waits for them, and re-layouts, local(): picked = thickness[:, asked]  119 us
    psum x1, blocking collectives, local(): products, sums, count = lax.psum((products, sums, count), ('gx', 'gy'))  77.4 us
    scatter x1, local copies, waits for them, and re-layouts, local(): slot_depart = jnp.zeros((slots_all,), jnp.float32).at[target].set(departure)  61.1 us
    scatter x1, local copies, waits for them, and re-layouts, local(): placed = jnp.full((3, slots_all), -1, jnp.int32).at[:, target].set(stacked)  47.4 us
    dot_general x8, matrix products, accumulate(): jnp.dot(outer, hits, precision=lax.Precision.HIGHEST, preferred_element_t...  36.2 us
    slice x1, other arithmetic, local(): slot_group = placed[2]  30.9 us
    mul x8, other arithmetic, accumulate(): block[:, None, :] * block[None, :, :]  19.2 us
    unnamed x5, waiting for transfers between devices  17.5 us
  transfers between devices with their start and end apart: 5, of which 4 were waited for; matrix products, arithmetic and copies ran while one was open for 13% of the time, Pallas kernels for 0%

commit v1 on v0

--- a/solution.py
+++ b/solution.py
@@ -87,7 +87,7 @@
         lax.psum_scatter(sums, "row", scatter_dimension=1, tiled=True),
         lax.psum_scatter(count, "row", scatter_dimension=1, tiled=True),
     )
-    products, sums, count = lax.psum((products, sums, count), ("gx", "gy"))
+    products, sums, count = lax.psum(lax.psum((products, sums, count), "gy"), "gx")
     scale = 1.0 / (count + 1.0)
     covariance = (products * scale).reshape(npred, npred, share)
     cross = sums * scale

time: 523 us -> 482 us (0.922)
  blocking collectives: 77.4 us -> 36.7 us
    psum x1 -> x2, blocking collectives: 77.4 us -> 36.7 us  [the longest x1 20.1 us: local(): lax.psum((products, sums, count), 'gy')]
  transfers between devices with their start and end apart: 5 -> 5, of which waited for: 4 -> 4; matrix products, arithmetic and copies ran while one was open for 13% -> 14% of each run, Pallas kernels for 0% -> 0%
where the time goes in v1:
time: 482 us; the launch traced here: 479 us
  local copies, waits for them, and re-layouts  268 us (56%)
  other arithmetic  57.9 us (12%)
  matrix products  51.1 us (11%)
  blocking collectives  36.7 us (8%)
  waiting for transfers between devices  33.7 us (7%)
  between operations  13.9 us (3%)
  starting transfers between devices  12.1 us (3%)
  loops' own time  5.87 us (1%)
    gather x2, local copies, waits for them, and re-layouts, local(): picked = thickness[:, asked]  119 us
    scatter x1, local copies, waits for them, and re-layouts, local(): slot_depart = jnp.zeros((slots_all,), jnp.float32).at[target].set(departure)  61.1 us
    scatter x1, local copies, waits for them, and re-layouts, local(): placed = jnp.full((3, slots_all), -1, jnp.int32).at[:, target].set(stacked)  47.4 us
    dot_general x8, matrix products, accumulate(): jnp.dot(outer, hits, precision=lax.Precision.HIGHEST, preferred_element_t...  36.2 us
    slice x1, other arithmetic, local(): slot_group = placed[2]  30.9 us
    psum x1, blocking collectives, local(): lax.psum((products, sums, count), 'gy')  20.1 us
    mul x8, other arithmetic, accumulate(): block[:, None, :] * block[None, :, :]  19.2 us
    unnamed x5, waiting for transfers between devices  17.5 us
  transfers between devices with their start and end apart: 5, of which 4 were waited for; matrix products, arithmetic and copies ran while one was open for 14% of the time, Pallas kernels for 0%

profile of v1, /device:TPU:0, one launch (start us, length us, event | category | flops | bytes accessed | tf_op | source)
XLA Modules:
  0.0 479.4 jit_solution(6794877788336958983)
XLA Ops:
  7.2 1.1 copy.35
  8.7 1.1 broadcast_add_fusion
  9.8 1.6 copy.36
  11.4 1.6 fusion.17
  13.0 0.9 compare_select_fusion.1
  14.0 1.1 add_bitcast_fusion
  15.1 5.1 %copy.37 = s32[16384,3]{1,0:T(8,128)} copy(s32[16384,3]{0,1:T(4,128)S(1)} %add_bitcast_fusion) | data formatting | bytes 393216 | tf_op jit(solution)/shard_map/stack | solution.py:32
  20.1 47.4 %scatter_custom_fusion = s32[3,32768]{0,1:T(8,128)} fusion(s32[16384]{0:T(1024)S(1)} %bitcast.78, s32[16384,3]{1,0:T(8,128)} %copy.37, s32[]{:T(128)} %constant.6.clone.1), kind=kCustom, calls=%fused_computation.26 | custom fusion | bytes 393728 | tf_op jit(solution)/shard_map/scatter | solution.py:33
  67.5 30.9 %slice_reduce_fusion = (s32[32768]{0:T(1024)}, s32[32768]{0:T(1024)}, s32[32768]{0:T(1024)}) fusion(s32[3,32768]{0,1:T(8,128)} %scatter_custom_fusion), kind=kLoop, calls=%fused_computation.21 | loop fusion | flops 32768 | bytes 786432 | tf_op jit(solution)/shard_map/slice | solution.py:44
  98.4 8.3 %all-to-all-start = ((s32[16,1,2048]{2,1,0:T(1,128)}), s32[16,1,2048]{2,1,0:T(1,128)S(1)}, u32[]{:S(2)}, u32[]{:S(2)}) async-start(s32[16,1,2048]{2,1,0:T(1,128)} %bitcast.24), calls=%async_computation | async-start | bytes 262144 | tf_op jit(solution)/shard_map/all_to_all | solution.py:11
  107.2 1.8 copy.39
  109.0 5.5 %all-to-all-done = s32[16,1,2048]{2,1,0:T(1,128)S(1)} async-done(((s32[16,1,2048]{2,1,0:T(1,128)}), s32[16,1,2048]{2,1,0:T(1,128)S(1)}, u32[]{:S(2)}, u32[]{:S(2)}) %all-to-all-start) | async-done | bytes 131104 | tf_op jit(solution)/shard_map/all_to_all | solution.py:11
  114.6 111.2 %gather_fusion = bf16[32768,16]{1,0:T(8,128)(2,1)} fusion(bf16[16,8192]{0,1:T(8,128)(2,1)} %copy.39, s32[32768]{0:T(1024)S(1)} %broadcast_clamp_fusion), kind=kCustom, calls=%fused_computation | custom fusion | bytes 2228224 | tf_op jit(solution)/shard_map/gather | solution.py:40
  225.8 7.8 %copy.40 = bf16[16,2048,16]{1,2,0:T(8,128)(2,1)} copy(bf16[16,2048,16]{2,1,0:T(8,128)(2,1)} %bitcast.64) | data formatting | bytes 2097152 | tf_op jit(solution)/shard_map/gather | solution.py:40
  233.6 3.7 all-to-all-start.1
  237.4 61.1 %scatter_custom_fusion.1 = f32[32768]{0:T(1024)} fusion(s32[16384]{0:T(1024)S(1)} %bitcast.79, f32[16384]{0:T(1024)} %param.17, f32[]{:T(128)} %constant.20.clone.1), kind=kCustom, calls=%fused_computation.41 | custom fusion | bytes 131584 | tf_op jit(solution)/shard_map/scatter | solution.py:34
  298.5 1.0 copy.47
  299.6 103.2 %while.15 = (s32[]{:T(128)}, f32[256,64]{0,1:T(8,128)S(1)}, f32[16,64]{1,0:T(8,128)}, f32[1,64]{1,0:T(1,128)S(1)}, s32[8]{0:T(128)S(1)}, /*index=5*/bf16[16,3276...) while((s32[]{:T(128)}, f32[256,64]{0,1:T(8,128)S(1)}, ...), condition=%wide.region_7.8_spmd.clone, body=%wide.region_5.7_spmd.clone.sunk | while | flops 883525696 | bytes 9661715 | solution.py:83
  300.9 0.7 dynamic_slice.29
  301.6 1.2 fusion.36
  302.8 2.4 broadcast_multiply_fusion.4
  306.0 4.5 convolution_add_fusion.4
  310.5 0.7 dynamic_slice.31
  313.8 0.7 dynamic_slice.29
  314.5 1.2 fusion.36
  315.7 2.4 broadcast_multiply_fusion.4
  318.9 4.5 convolution_add_fusion.4
  323.4 0.7 dynamic_slice.31
  326.7 0.7 dynamic_slice.29
  327.4 1.2 fusion.36
  328.6 2.4 broadcast_multiply_fusion.4
  331.8 4.5 convolution_add_fusion.4
  336.3 0.7 dynamic_slice.31
  339.6 0.7 dynamic_slice.29
  340.3 1.2 fusion.36
  341.5 2.4 broadcast_multiply_fusion.4
  344.7 4.5 convolution_add_fusion.4
  349.2 0.7 dynamic_slice.31
  352.5 0.7 dynamic_slice.29
  353.2 1.2 fusion.36
  354.4 2.4 broadcast_multiply_fusion.4
  357.6 4.5 convolution_add_fusion.4
  362.1 0.7 dynamic_slice.31
  365.4 0.7 dynamic_slice.29
  366.1 1.2 fusion.36
  367.3 2.4 broadcast_multiply_fusion.4
  370.5 4.5 convolution_add_fusion.4
  375.0 0.7 dynamic_slice.31
  378.3 0.7 dynamic_slice.29
  379.0 1.2 fusion.36
  380.2 2.4 broadcast_multiply_fusion.4
  383.4 4.5 convolution_add_fusion.4
  391.9 1.2 fusion.36
  393.1 2.4 broadcast_multiply_fusion.4
  396.3 4.5 convolution_add_fusion.4
  403.5 1.4 copy.45
  405.7 6.7 %reduce-scatter.10.cloned.1.call-done = f32[32,1]{1,0:T(8,128)} async-done(((f32[64,1]{1,0:T(8,128)}), f32[32,1]{1,0:T(8,128)}) %reduce-scatter.10.cloned.1.call-update) | async-done | bytes 144
  412.4 0.8 copy.44
  413.2 10.1 %reduce-scatter.12.cloned.1.call-done = f32[32,16]{1,0:T(8,128)} async-done(((f32[64,16]{1,0:T(8,128)}), f32[32,16]{1,0:T(8,128)}) %reduce-scatter.12.cloned.1.call-update) | async-done | bytes 2064
  423.3 0.8 copy.46
  424.1 10.7 %reduce-scatter.8.cloned.1.call-done = f32[256,32]{0,1:T(8,128)} async-done(((f32[256,64]{0,1:T(8,128)}), f32[256,32]{0,1:T(8,128)}) %reduce-scatter.8.cloned.1.call-update) | async-done | bytes 32784 | tf_op jit(solution)/shard_map/reduce_scatter | solution.py:86
  434.7 20.1 %all-reduce = (f32[256,32]{0,1:T(8,128)S(1)}, f32[1,32]{1,0:T(1,128)S(1)}, f32[16,32]{1,0:T(8,128)S(1)}) all-reduce(f32[256,32]{0,1:T(8,128)} %reduce-scatter.8.cloned.1.call-done, f32[1,32]{1,0:T(1,128)S(1)} %copy.44, f32[16,32]{1,0:T(8,128)S(1)} %copy.46), channel_id=1, replica_groups=mesh['gx'=4,'gy'=4,'row'=2] {'gy'}, use_global_device_ids=true, to_apply=%region_9.10 | all-reduce | flops 8736 | bytes 69888 | tf_op jit(solution)/shard_map/psum | solution.py:90
  454.8 16.6 %all-reduce.1 = (f32[256,32]{0,1:T(8,128)S(1)}, f32[1,32]{1,0:T(1,128)S(1)}, f32[16,32]{1,0:T(8,128)S(1)}) all-reduce(f32[256,32]{0,1:T(8,128)S(1)} %get-tuple-element.129, f32[1,32]{1,0:T(1,128)S(1)} %get-tuple-element.130, f32[16,32]{1,0:T(8,128)S(1)} %get-tuple-element.131), channel_id=1, replica_groups=mesh['gx'=4,'gy'=4,'row'=2] {'gx'}, use_global_device_ids=true, to_apply=%region_10.11 | all-reduce | flops 8736 | bytes 69888 | tf_op jit(solution)/shard_map/psum | solution.py:90
  472.1 0.8 copy.42
  (106 shorter events, 26.3 us)
Async XLA Ops:
  7.2 99.6 %copy-start = (bf16[137,8192]{1,0:T(8,128)(2,1)S(1)}, bf16[137,8192]{1,0:T(8,128)(2,1)}, u32[]{:S(2)}) copy-start(bf16[137,8192]{1,0:T(8,128)(2,1)} %param.10) | copy-start | bytes 6733828
  67.5 39.3 %copy-start.3 = (bf16[137,16]{0,1:T(8,128)(2,1)S(1)}, bf16[137,16]{0,1:T(8,128)(2,1)}, u32[]{:S(2)}) copy-start(bf16[137,16]{0,1:T(8,128)(2,1)} %param.11) | copy-start | bytes 13156
  98.4 16.0 %all-to-all-start = ((s32[16,1,2048]{2,1,0:T(1,128)}), s32[16,1,2048]{2,1,0:T(1,128)S(1)}, u32[]{:S(2)}, u32[]{:S(2)}) async-start(s32[16,1,2048]{2,1,0:T(1,128)} %bitcast.24), calls=%async_computation | async-start | bytes 262144 | tf_op jit(solution)/shard_map/all_to_all | solution.py:11
  225.8 73.7 %copy-start.2 = (f32[16,32]{1,0:T(8,128)S(1)}, f32[16,32]{1,0:T(8,128)}, u32[]{:S(2)}) copy-start(f32[16,32]{1,0:T(8,128)} %param.12) | copy-start | bytes 6148
  233.6 64.9 %all-to-all-start.1 = ((bf16[16,16,2048]{2,0,1:T(8,128)(2,1)}), bf16[16,16,2048]{2,0,1:T(8,128)(2,1)S(1)}, u32[]{:S(2)}, u32[]{:S(2)}) async-start(bf16[16,16,2048]{2,0,1:T(8,128)(2,1)} %bitcast.13), calls=%async_computation.1 | async-start | bytes 2097152 | tf_op jit(solution)/shard_map/all_to_all | solution.py:15
  237.3 175.1 %reduce-scatter.10.cloned.1.call-start = ((), (), s32[]{:S(2)}) async-start(), calls=%async_computation.6 | async-start | bytes 49152
  299.6 11.7 %copy-start.4 = (f32[16,64]{1,0:T(8,128)S(1)}, f32[16,64]{1,0:T(8,128)}, u32[]{:S(2)}) copy-start(f32[16,64]{1,0:T(8,128)} %get-tuple-element.212) | copy-start | bytes 12292 | tf_op jit(solution)/shard_map/while
  311.8 0.6 copy-start.5
  312.5 11.7 %copy-start.4 = (f32[16,64]{1,0:T(8,128)S(1)}, f32[16,64]{1,0:T(8,128)}, u32[]{:S(2)}) copy-start(f32[16,64]{1,0:T(8,128)} %get-tuple-element.212) | copy-start | bytes 12292 | tf_op jit(solution)/shard_map/while
  324.7 0.6 copy-start.5
  325.4 11.7 %copy-start.4 = (f32[16,64]{1,0:T(8,128)S(1)}, f32[16,64]{1,0:T(8,128)}, u32[]{:S(2)}) copy-start(f32[16,64]{1,0:T(8,128)} %get-tuple-element.212) | copy-start | bytes 12292 | tf_op jit(solution)/shard_map/while
  337.6 0.6 copy-start.5
  338.2 11.7 %copy-start.4 = (f32[16,64]{1,0:T(8,128)S(1)}, f32[16,64]{1,0:T(8,128)}, u32[]{:S(2)}) copy-start(f32[16,64]{1,0:T(8,128)} %get-tuple-element.212) | copy-start | bytes 12292 | tf_op jit(solution)/shard_map/while
  350.5 0.6 copy-start.5
  351.1 11.7 %copy-start.4 = (f32[16,64]{1,0:T(8,128)S(1)}, f32[16,64]{1,0:T(8,128)}, u32[]{:S(2)}) copy-start(f32[16,64]{1,0:T(8,128)} %get-tuple-element.212) | copy-start | bytes 12292 | tf_op jit(solution)/shard_map/while
  363.4 0.6 copy-start.5
  364.1 11.7 %copy-start.4 = (f32[16,64]{1,0:T(8,128)S(1)}, f32[16,64]{1,0:T(8,128)}, u32[]{:S(2)}) copy-start(f32[16,64]{1,0:T(8,128)} %get-tuple-element.212) | copy-start | bytes 12292 | tf_op jit(solution)/shard_map/while
  376.3 0.6 copy-start.5
  376.9 11.7 %copy-start.4 = (f32[16,64]{1,0:T(8,128)S(1)}, f32[16,64]{1,0:T(8,128)}, u32[]{:S(2)}) copy-start(f32[16,64]{1,0:T(8,128)} %get-tuple-element.212) | copy-start | bytes 12292 | tf_op jit(solution)/shard_map/while
  389.2 0.6 copy-start.5
  389.8 11.7 %copy-start.4 = (f32[16,64]{1,0:T(8,128)S(1)}, f32[16,64]{1,0:T(8,128)}, u32[]{:S(2)}) copy-start(f32[16,64]{1,0:T(8,128)} %get-tuple-element.212) | copy-start | bytes 12292 | tf_op jit(solution)/shard_map/while
  402.1 0.6 copy-start.5
  402.7 2.2 copy-start.1
  403.5 19.8 %reduce-scatter.12.cloned.1.call-start = ((), (), s32[]{:S(2)}) async-start(), calls=%async_computation.7 | async-start | bytes 49152
  404.9 29.8 %reduce-scatter.8.cloned.1.call-start = ((), (), s32[]{:S(2)}) async-start(), calls=%async_computation.5 | async-start | bytes 98304 | tf_op jit(solution)/shard_map/reduce_scatter | solution.py:86
Sparse Core Ops, SparseCore 0:
  403.6 8.7 reduce-scatter.9
  414.6 8.6 reduce-scatter.11
  426.0 8.6 reduce-scatter.7
